TPU v7x, 256 devices: a whole 4x4x8 slice. The times are simulated.
256 devices in a mesh: dp: 8 (over x, y_lo), expert: 16 (over z, core), tensor: 2 (over y_hi).
Axes of the slice: x: 4, y: 4 (y_hi: 2, y_lo: 2; y = y_hi * 2 + y_lo), z: 8, core: 2. Of those that a mesh axis runs over, the one named last changes fastest.
Arguments:
- tokens: bfloat16 [1536, 256, 1280], P(('dp', 'expert', 'tensor')), may hold values from -16 to 16
- cotangent: bfloat16 [1536, 256, 1280], P(('dp', 'expert', 'tensor')), may hold values from -6 to 6
- norm_gain: float32 [1280], replicated, may hold values from 0.5 to 1.5
- slot_keys: bfloat16 [1280, 32], replicated, may hold values from -2 to 2
- w_in: bfloat16 [16, 1280, 2560], P('expert', None, 'tensor'), may hold values from -0.15625 to 0.15625
- w_out: bfloat16 [16, 2560, 1280], P('expert', 'tensor'), may hold values from -0.125 to 0.125
Outputs:
- grad_tokens: bfloat16 [1536, 256, 1280], P(('dp', 'expert', 'tensor'))
- grad_gain: float32 [1280], replicated
- grad_keys: float32 [1280, 32], replicated
- grad_in: bfloat16 [16, 1280, 2560], P('expert', 'dp', 'tensor')
- grad_out: bfloat16 [16, 2560, 1280], P('expert', 'tensor', 'dp')
All inputs are finite; a program needn't handle non-finite values.
Results may differ from a plain program's by a relative error of at most 0.014.
The roundings to bfloat16 on the way count: a program that leaves them out, or rounds other values in their place, can miss the bound.
Values may be sent and summed in bfloat16 or wider, within the bound.
No kernel may reach another device: no remote copies, remote signals or barrier semaphores. Data moves between devices by JAX's collectives and lax.ppermute only.
A program may use at most 128 MiB of HBM per device.

v0:
```python
import jax
import jax.numpy as jnp
from jax import lax
from jax.sharding import PartitionSpec as P

SLOT_PER = 2
EPSILON = 1e-06


def from_everyone(shard, axis):
    devices = lax.axis_size(axis)
    return lax.all_to_all(
        jnp.broadcast_to(shard[None], (devices, *shard.shape)), axis, 0, 0, tiled=True
    )


def in_order(tiles, dim):
    shape = list(tiles.shape[1:])
    shape[dim] *= tiles.shape[0]
    return jnp.moveaxis(tiles, 0, dim).reshape(shape)


def collect(shard, axis, dim):
    tiles = from_everyone(shard, axis)
    return in_order(tiles, dim)


def in_blocks(shard, dim, devices):
    before, after = (shard.shape[:dim], shard.shape[dim + 1 :])
    return jnp.moveaxis(shard.reshape(*before, devices, -1, *after), dim, 0)


def summed_on_arrival(shard, axis, dim):
    tiles = in_blocks(shard, dim, lax.axis_size(axis))
    arrived = lax.all_to_all(tiles, axis, split_axis=0, concat_axis=0, tiled=True)
    return arrived.sum(axis=0)


def sent_and_summed(shard, axis, dim):
    devices = lax.axis_size(axis)
    tiles = lax.all_to_all(in_blocks(shard, dim, devices), axis, 0, 0, tiled=True)
    return jnp.sum(tiles.astype(jnp.float32), axis=0)


def mixing_forward(tokens, gain, slot_keys):
    average = jnp.mean(tokens, axis=-1, keepdims=True, dtype=jnp.float32)
    centred = tokens.astype(jnp.float32) - average
    spread = jnp.mean(centred * centred, axis=-1, keepdims=True)
    inverse = lax.rsqrt(spread + EPSILON)
    scaled = centred * inverse
    normed = (scaled * gain).astype(jnp.bfloat16)
    logits = jnp.einsum("bmd,dn->bmn", normed, slot_keys, preferred_element_type=jnp.float32)
    dispatch = jax.nn.softmax(logits, axis=1)
    combine = jax.nn.softmax(logits, axis=2)
    dispatch_low = dispatch.astype(jnp.bfloat16)
    slot_values = jnp.einsum(
        "bmn,bmd->bnd", dispatch_low, normed, preferred_element_type=jnp.float32
    )
    return (slot_values, combine, (scaled, inverse, normed, dispatch, combine, dispatch_low))


def mixing_backward(saved, gain, slot_keys, slot_grad, combine_grad):
    scaled, inverse, normed, dispatch, combine, dispatch_low = saved
    grad_dispatch = jnp.einsum(
        "bnd,bmd->bmn", slot_grad, normed, preferred_element_type=jnp.float32
    )
    grad_normed = jnp.einsum(
        "bmn,bnd->bmd", dispatch_low, slot_grad, preferred_element_type=jnp.float32
    )
    grad_logits = dispatch * (
        grad_dispatch - jnp.sum(dispatch * grad_dispatch, axis=1, keepdims=True)
    )
    grad_logits = grad_logits + combine * (
        combine_grad - jnp.sum(combine * combine_grad, axis=2, keepdims=True)
    )
    keys_wide = slot_keys.astype(jnp.float32)
    grad_normed = grad_normed + jnp.einsum(
        "bmn,dn->bmd", grad_logits, keys_wide, precision=lax.Precision.HIGHEST
    )
    keys_term = jnp.einsum(
        "bmd,bmn->dn", normed.astype(jnp.float32), grad_logits, precision=lax.Precision.HIGHEST
    )
    gain_term = jnp.sum(grad_normed * scaled, axis=(0, 1))
    grad_scaled = grad_normed * gain
    first_mean = jnp.mean(grad_scaled, axis=-1, keepdims=True)
    second_mean = jnp.mean(grad_scaled * scaled, axis=-1, keepdims=True)
    grad_tok = inverse * (grad_scaled - first_mean - scaled * second_mean)
    return (grad_tok, gain_term, keys_term)


def contract_rows(left, right):
    return lax.dot_general(
        left, right, (((0,), (0,)), ((), ())), preferred_element_type=jnp.float32
    )


def contract_cols(left, right):
    return lax.dot_general(
        left, right, (((1,), (1,)), ((), ())), preferred_element_type=jnp.float32
    )


def local(tokens, cotangent, norm_gain, slot_keys, w_in, w_out):
    local_imgs, token_count, features = tokens.shape
    slot_count = slot_keys.shape[1]
    experts = slot_count // SLOT_PER
    slot_values, combine, saved = mixing_forward(tokens, norm_gain, slot_keys)
    slot_inputs = slot_values.astype(jnp.bfloat16).reshape(local_imgs, experts, SLOT_PER, features)
    arrived = lax.all_to_all(slot_inputs, "expert", split_axis=1, concat_axis=0, tiled=True)
    slot_rows = collect(arrived, "tensor", 0).reshape(-1, features)
    first_proj = w_in[0]
    second_proj = w_out[0]
    pre_act = jnp.dot(slot_rows, first_proj, preferred_element_type=jnp.float32)
    hidden = jax.nn.gelu(pre_act).astype(jnp.bfloat16)
    segment = hidden
    outputs = summed_on_arrival(
        jnp.dot(segment, second_proj, preferred_element_type=jnp.float32), "tensor", 0
    )
    outputs = outputs.astype(jnp.bfloat16).reshape(arrived.shape)
    returned = lax.all_to_all(outputs, "expert", split_axis=0, concat_axis=1, tiled=True).reshape(
        local_imgs, slot_count, features
    )
    combine_low = combine.astype(jnp.bfloat16)
    grad_slots = jnp.einsum(
        "bmn,bmd->bnd", combine_low, cotangent, preferred_element_type=jnp.float32
    )
    grad_slots = grad_slots.astype(jnp.bfloat16).reshape(local_imgs, experts, SLOT_PER, features)
    grad_combine = jnp.einsum(
        "bmd,bnd->bmn", cotangent, returned, preferred_element_type=jnp.float32
    )
    grads_sent = lax.all_to_all(grad_slots, "expert", split_axis=1, concat_axis=0, tiled=True)
    grad_rows = collect(grads_sent, "tensor", 0).reshape(-1, features)
    grad_hidden = contract_cols(grad_rows, second_proj)
    grad_pre = jax.vjp(jax.nn.gelu, pre_act)[1](grad_hidden)[0].astype(jnp.bfloat16)
    segment = grad_pre
    grad_in_rows = sent_and_summed(
        contract_cols(segment, first_proj).astype(jnp.bfloat16), "tensor", 0
    )
    grad_in_rows = grad_in_rows.astype(jnp.bfloat16).reshape(arrived.shape)
    grad_back = lax.all_to_all(
        grad_in_rows, "expert", split_axis=0, concat_axis=1, tiled=True
    ).reshape(local_imgs, slot_count, features)
    grad_tok, gain_term, keys_term = mixing_backward(
        saved, norm_gain, slot_keys, grad_back, grad_combine
    )
    grad_tokens = (cotangent.astype(jnp.float32) + grad_tok).astype(jnp.bfloat16)
    grad_gain, grad_keys = lax.psum((gain_term, keys_term), ("dp", "expert", "tensor"))
    columns = slot_rows
    grad_first = lax.psum_scatter(
        contract_rows(columns, grad_pre).astype(jnp.bfloat16), "dp", scatter_dimension=0, tiled=True
    )
    columns = grad_rows
    grad_second = (
        lax.psum_scatter(
            contract_rows(columns, hidden).astype(jnp.bfloat16),
            "dp",
            scatter_dimension=0,
            tiled=True,
        )
        .astype(jnp.float32)
        .T
    )
    return (
        grad_tokens,
        grad_gain,
        grad_keys,
        grad_first[None],
        grad_second.astype(jnp.bfloat16)[None],
    )


def solution(mesh):
    placed = (
        P(("dp", "expert", "tensor"), None, None),
        P(("dp", "expert", "tensor"), None, None),
        P(),
        P(),
        P("expert", None, "tensor"),
        P("expert", "tensor", None),
    )
    return jax.shard_map(
        local,
        mesh=mesh,
        in_specs=placed,
        out_specs=(
            P(("dp", "expert", "tensor"), None, None),
            P(),
            P(),
            P("expert", "dp", "tensor"),
            P("expert", "tensor", "dp"),
        ),
        check_vma=False,
    )
```

profile of v0, /device:TPU:1, one launch (start us, length us, event | category | flops | bytes accessed | tf_op | source)
XLA Modules:
  0.0 502.3 jit_solution(15583305845671244630)
XLA Ops:
  15.5 3.8 convolution_convert_fusion.3
  23.5 10.0 %all-to-all-start = ((bf16[6,16,2,1280]{3,2,0,1:T(2,128)(2,1)}), bf16[6,16,2,1280]{3,2,0,1:T(2,128)(2,1)}, u32[]{:S(2)}, u32[]{:S(2)}) async-start(bf16[6,16,2,1280]{3,2,0,1:T(2,128)(2,1)} %copy.15), calls=%async_computation | async-start | bytes 983040 | tf_op jit(solution)/shard_map/all_to_all | solution.py:131
  35.2 4.6 convolution_convert_fusion.2
  44.0 6.1 %all-to-all-done = bf16[6,16,2,1280]{3,2,0,1:T(2,128)(2,1)} async-done(((bf16[6,16,2,1280]{3,2,0,1:T(2,128)(2,1)}), bf16[6,16,2,1280]{3,2,0,1:T(2,128)(2,1)}, u32[]{:S(2)}, u32[]{:S(2)}) %all-to-all-start) | async-done | bytes 491552 | tf_op jit(solution)/shard_map/all_to_all | solution.py:131
  50.1 19.4 %all_to_all.80 = bf16[6,16,2,1280]{3,2,0,1:T(2,128)(2,1)S(1)} all-to-all(bf16[6,16,2,1280]{3,2,0,1:T(2,128)(2,1)} %copy.16), channel_id=1, replica_groups=mesh['dp'=8,'expert'=16,'tensor'=2] {'expert'}, dimensions={1} | all-to-all | bytes 983040 | tf_op jit(solution)/shard_map/all_to_all | solution.py:109
  70.0 18.9 %all_to_all.81 = bf16[2,96,1,2,1280]{4,3,2,1,0:T(2,128)(2,1)} all-to-all(bf16[2,96,1,2,1280]{4,3,2,1,0:T(2,128)(2,1)S(1)} %broadcast_in_dim.15), channel_id=1, replica_groups=mesh['dp'=8,'expert'=16,'tensor'=2] {'tensor'}, dimensions={0} | all-to-all | bytes 1966080 | tf_op jit(solution)/shard_map/all_to_all | solution.py:12
  91.4 4.6 all-to-all-start.1
  99.3 4.4 multiply_convert_fusion
  103.7 6.3 %all-to-all-done.1 = bf16[2,96,1,2,1280]{4,3,2,1,0:T(2,128)(2,1)} async-done(((bf16[2,96,1,2,1280]{4,3,2,1,0:T(2,128)(2,1)}), bf16[2,96,1,2,1280]{4,3,2,1,0:T(2,128)(2,1)}, u32[]{:S(2)}, u32[]{:S(2)}) %all-to-all-start.1) | async-done | bytes 983072 | tf_op jit(solution)/shard_map/all_to_all | solution.py:12
  113.3 4.9 fusion.33
  124.2 4.9 fusion.16
  129.2 8.3 %all-to-all-done.4 = bf16[2,192,1280]{2,1,0:T(8,128)(2,1)S(1)} async-done(((bf16[2,192,1280]{2,1,0:T(8,128)(2,1)}), bf16[2,192,1280]{2,1,0:T(8,128)(2,1)S(1)}, u32[]{:S(2)}, u32[]{:S(2)}) %all-to-all-start.4) | async-done | bytes 983072 | tf_op jit(solution)/shard_map/all_to_all | solution.py:41
  137.5 3.7 all-to-all-start.6
  144.3 19.8 %all-to-all-done.6 = f32[2,192,1280]{2,1,0:T(8,128)S(1)} async-done(((f32[2,192,1280]{2,1,0:T(8,128)}), f32[2,192,1280]{2,1,0:T(8,128)S(1)}, u32[]{:S(2)}, u32[]{:S(2)}) %all-to-all-start.6) | async-done | bytes 1966112 | tf_op jit(solution)/shard_map/all_to_all | solution.py:35
  164.1 6.3 %all-to-all-start.5 = ((bf16[96,1,2,1280]{3,2,1,0:T(2,128)(2,1)}), bf16[96,1,2,1280]{3,2,1,0:T(2,128)(2,1)S(1)}, u32[]{:S(2)}, u32[]{:S(2)}) async-start(bf16[96,1,2,1280]{3,2,1,0:T(2,128)(2,1)} %reshape.82), calls=%async_computation.5 | async-start | bytes 983040 | tf_op jit(solution)/shard_map/all_to_all | solution.py:140
  171.5 15.6 %all-to-all-done.5 = bf16[96,1,2,1280]{3,2,1,0:T(2,128)(2,1)S(1)} async-done(((bf16[96,1,2,1280]{3,2,1,0:T(2,128)(2,1)}), bf16[96,1,2,1280]{3,2,1,0:T(2,128)(2,1)S(1)}, u32[]{:S(2)}, u32[]{:S(2)}) %all-to-all-start.5) | async-done | bytes 491552 | tf_op jit(solution)/shard_map/all_to_all | solution.py:140
  194.8 11.7 %all-to-all-done.7 = bf16[96,1,2,1280]{3,2,1,0:T(2,128)(2,1)S(1)} async-done(((bf16[96,1,2,1280]{3,2,1,0:T(2,128)(2,1)}), bf16[96,1,2,1280]{3,2,1,0:T(2,128)(2,1)S(1)}, u32[]{:S(2)}, u32[]{:S(2)}) %all-to-all-start.7) | async-done | bytes 491552 | tf_op jit(solution)/shard_map/all_to_all | solution.py:120
  213.7 5.0 convolution_convert_fusion.1
  219.0 4.9 convolution_convert_fusion
  224.0 5.6 %fusion.44 = f32[6,256,1280]{2,1,0:T(8,128)} fusion(bf16[6,32,1280]{2,1,0:T(8,128)(2,1)S(1)} %reshape.83, f32[6,32]{1,0:T(8,128)S(1)} %get-tuple-element.8, f32[6,256,32]{1,2,0:T(8,128)} %copy-done.4), kind=kOutput, calls=%fused_computation.58 | convolution fusion | flops 125977024 | bytes 8553216 | tf_op jit(solution)/shard_map/bmn,bnd->bmd/dot_general | solution.py:67
  229.6 10.7 %fusion.14 = (f32[1280]{0:T(1024)S(1)}, f32[6,256]{1,0:T(8,128)S(1)}, f32[6,256]{1,0:T(8,128)S(1)}, f32[6,256,1280]{2,1,0:T(8,128)}) fusion(bf16[6,256,1280]{2,1,0:T(8,128)(2,1)} %param.6, f32[6,256]{1,0:T(8,128)S(1)} %add_rsqrt_fusion, f32[6,256]{1,0:T(8,128)S(1)} %broadcast_multiply_fusion.2, f32[1280]{0:T(1024)S(1)} %copy-done.10, ...), kind=kOutput, calls=%fused_computation.16 | convolution fusion | flops 774631168 | bytes 19974144 | tf_op jit(solution)/shard_map/bmn,dn->bmd/dot_general | solution.py:77
  240.2 79.7 %psum.14 = f32[1280]{0:T(1024)} all-reduce(f32[1280]{0:T(1024)S(1)} %get-tuple-element.5), channel_id=1, replica_groups=mesh['dp'=8,'expert'=16,'tensor'=2] {'dp','expert','tensor'}, use_global_device_ids=true, to_apply=%region_13.0 | all-reduce | flops 1280 | bytes 10240 | tf_op jit(solution)/shard_map/psum | solution.py:147
  319.9 8.7 %fusion.13 = bf16[6,256,1280]{2,1,0:T(8,128)(2,1)} fusion(bf16[6,256,1280]{2,1,0:T(8,128)(2,1)} %param.6, bf16[6,256,1280]{2,1,0:T(8,128)(2,1)} %param.7, f32[6,256,1280]{2,1,0:T(8,128)} %get-tuple-element.18, f32[6,256]{1,0:T(8,128)S(1)} %get-tuple-element.19, f32[6,256]{1,0:T(8,128)S(1)} %get-tuple-element.20, f32[1280]{0:T(1024)S(1)} %copy-done.10, ...), kind=kLoop, calls=%fused_computation.15 | loop fusion | flops 21626880 | bytes 19690496 | tf_op jit(solution)/shard_map/convert_element_type | solution.py:146
  328.6 164.7 %all-reduce.2.cloned.1.call-done = f32[1280,32]{0,1:T(8,128)} async-done(((f32[1280,32]{0,1:T(8,128)}), f32[1280,32]{0,1:T(8,128)}) %all-reduce.2.cloned.1.call-update) | async-done | bytes 163856 | tf_op jit(solution)/shard_map/psum | solution.py:147
  (64 shorter events, 54.1 us)
Async XLA Ops:
  8.0 91.3 %copy-start = (bf16[1,1280,1280]{2,1,0:T(8,128)(2,1)S(1)}, bf16[1,1280,1280]{2,1,0:T(8,128)(2,1)}, u32[]{:S(2)}) copy-start(bf16[1,1280,1280]{2,1,0:T(8,128)(2,1)} %param.10) | copy-start | bytes 9830404
  8.0 3.4 copy-start.2
  8.0 4.6 copy-start.10
  8.0 4.6 copy-start.8
  14.4 0.7 copy-start.4
  23.5 26.6 %all-to-all-start = ((bf16[6,16,2,1280]{3,2,0,1:T(2,128)(2,1)}), bf16[6,16,2,1280]{3,2,0,1:T(2,128)(2,1)}, u32[]{:S(2)}, u32[]{:S(2)}) async-start(bf16[6,16,2,1280]{3,2,0,1:T(2,128)(2,1)} %copy.15), calls=%async_computation | async-start | bytes 983040 | tf_op jit(solution)/shard_map/all_to_all | solution.py:131
  91.4 18.6 %all-to-all-start.1 = ((bf16[2,96,1,2,1280]{4,3,2,1,0:T(2,128)(2,1)}), bf16[2,96,1,2,1280]{4,3,2,1,0:T(2,128)(2,1)}, u32[]{:S(2)}, u32[]{:S(2)}) async-start(bf16[2,96,1,2,1280]{4,3,2,1,0:T(2,128)(2,1)} %broadcast_in_dim.13), calls=%async_computation.1 | async-start | bytes 1966080 | tf_op jit(solution)/shard_map/all_to_all | solution.py:12
  118.2 2.4 copy-start.11
  120.7 16.8 %all-to-all-start.4 = ((bf16[2,192,1280]{2,1,0:T(8,128)(2,1)}), bf16[2,192,1280]{2,1,0:T(8,128)(2,1)S(1)}, u32[]{:S(2)}, u32[]{:S(2)}) async-start(bf16[2,192,1280]{2,1,0:T(8,128)(2,1)} %bitcast.77), calls=%async_computation.4 | async-start | bytes 1966080 | tf_op jit(solution)/shard_map/all_to_all | solution.py:41
  137.5 26.6 %all-to-all-start.6 = ((f32[2,192,1280]{2,1,0:T(8,128)}), f32[2,192,1280]{2,1,0:T(8,128)S(1)}, u32[]{:S(2)}, u32[]{:S(2)}) async-start(f32[2,192,1280]{2,1,0:T(8,128)} %fusion.16), calls=%async_computation.6 | async-start | bytes 3932160 | tf_op jit(solution)/shard_map/all_to_all | solution.py:35
  144.3 47.1 %copy-start.7 = (f32[6,256,32]{1,2,0:T(8,128)S(1)}, f32[6,256,32]{1,2,0:T(8,128)}, u32[]{:S(2)}) copy-start(f32[6,256,32]{1,2,0:T(8,128)} %get-tuple-element.9) | copy-start | bytes 589828
  164.1 23.0 %all-to-all-start.5 = ((bf16[96,1,2,1280]{3,2,1,0:T(2,128)(2,1)}), bf16[96,1,2,1280]{3,2,1,0:T(2,128)(2,1)S(1)}, u32[]{:S(2)}, u32[]{:S(2)}) async-start(bf16[96,1,2,1280]{3,2,1,0:T(2,128)(2,1)} %reshape.82), calls=%async_computation.5 | async-start | bytes 983040 | tf_op jit(solution)/shard_map/all_to_all | solution.py:140
  187.1 19.4 %all-to-all-start.7 = ((bf16[96,1,2,1280]{3,2,1,0:T(2,128)(2,1)}), bf16[96,1,2,1280]{3,2,1,0:T(2,128)(2,1)S(1)}, u32[]{:S(2)}, u32[]{:S(2)}) async-start(bf16[96,1,2,1280]{3,2,1,0:T(2,128)(2,1)} %convert_element_type.73), calls=%async_computation.7 | async-start | bytes 983040 | tf_op jit(solution)/shard_map/all_to_all | solution.py:120
  190.5 302.7 %all-reduce.2.cloned.1.call-start = ((), (), s32[]{:S(2)}) async-start(), calls=%async_computation.10 | async-start | bytes 327680 | tf_op jit(solution)/shard_map/psum | solution.py:147
  207.0 3.7 copy-start.3
  210.7 3.0 copy-start.6
  213.6 5.4 %copy-start.5 = (bf16[384,1280]{1,0:T(8,128)(2,1)S(1)}, bf16[384,1280]{1,0:T(8,128)(2,1)}, u32[]{:S(2)}) copy-start(bf16[384,1280]{1,0:T(8,128)(2,1)} %reshape_reshape.6) | copy-start | bytes 2949124
  213.7 279.6 %reduce-scatter.3.cloned.1.call-start = ((), (), s32[]{:S(2)}) async-start(), calls=%async_computation.11 | async-start | bytes 3686400 | tf_op jit(solution)/shard_map/reduce_scatter | solution.py:149
  218.7 274.5 %reduce-scatter.5.cloned.1.call-start = ((), (), s32[]{:S(2)}) async-start(), calls=%async_computation.12 | async-start | bytes 3686400 | tf_op jit(solution)/shard_map/reduce_scatter | solution.py:154
  224.0 5.6 %copy-start.9 = (bf16[1280,32]{0,1:T(8,128)(2,1)S(1)}, bf16[1280,32]{0,1:T(8,128)(2,1)}, u32[]{:S(2)}) copy-start(bf16[1280,32]{0,1:T(8,128)(2,1)} %param.9) | copy-start | bytes 245764
  319.9 174.9 %copy-start.1 = (bf16[1,1280,1280]{2,1,0:T(8,128)(2,1)S(1)}, bf16[1,1280,1280]{2,1,0:T(8,128)(2,1)}, u32[]{:S(2)}) copy-start(bf16[1,1280,1280]{2,1,0:T(8,128)(2,1)} %param.10) | copy-start | bytes 9830404
Sparse Core Ops, SparseCore 0:
  213.8 279.4 all-reduce.1
Sparse Core Ops, SparseCore 1:
  218.8 71.0 reduce-scatter.2
  292.9 76.7 reduce-scatter.4
where the time goes:
time: 504 us; the launch traced here: 502 us
  waiting for transfers between devices  232 us (46%)
  blocking collectives  118 us (23%)
  matrix products  62.9 us (12%)
  starting transfers between devices  32.3 us (6%)
  local copies, waits for them, and re-layouts  24.8 us (5%)
  other arithmetic  16.2 us (3%)
  between operations  15.7 us (3%)
    psum x1, waiting for transfers between devices, local(): lax.psum((gain_term, keys_term), ('dp', 'expert', 'tensor'))  165 us
    psum x1, blocking collectives, local(): lax.psum((gain_term, keys_term), ('dp', 'expert', 'tensor'))  79.7 us
    all_to_all x1, waiting for transfers between devices, summed_on_arrival(): lax.all_to_all(tiles, axis, split_axis=0, concat_axis=0, tiled=True)  19.8 us
    all_to_all x1, blocking collectives, local(): lax.all_to_all(slot_inputs, 'expert', split_axis=1, concat_axis=0, tiled=...  19.4 us
    all_to_all x1, blocking collectives, from_everyone(): lax.all_to_all(jnp.broadcast_to(shard[None], (devices, *shard.shape)), ax...  18.9 us
    all_to_all x1, waiting for transfers between devices, local(): lax.all_to_all(grad_in_rows, 'expert', split_axis=0, concat_axis=1, tiled...  15.6 us
    all_to_all x1, waiting for transfers between devices, local(): lax.all_to_all(outputs, 'expert', split_axis=0, concat_axis=1, tiled=True)  11.7 us
    dot_general x1, matrix products, mixing_backward(): jnp.einsum('bmn,dn->bmd', grad_logits, keys_wide, precision=lax.Precision...  10.7 us
  transfers between devices with their start and end apart: 9, of which 7 were waited for; matrix products, arithmetic and copies ran while one was open for 13% of the time, Pallas kernels for 0%

commit v1 on v0

--- a/solution.py
+++ b/solution.py
@@ -5,6 +5,11 @@
 
 SLOT_PER = 2
 EPSILON = 1e-06
+
+
+def _serve_records(x_in, ax_name, mesh_ax):
+    response = lax.psum(lax.psum(x_in, ax_name), mesh_ax)
+    return response
 
 
 def from_everyone(shard, axis):
@@ -144,7 +149,7 @@
         saved, norm_gain, slot_keys, grad_back, grad_combine
     )
     grad_tokens = (cotangent.astype(jnp.float32) + grad_tok).astype(jnp.bfloat16)
-    grad_gain, grad_keys = lax.psum((gain_term, keys_term), ("dp", "expert", "tensor"))
+    grad_gain, grad_keys = _serve_records((gain_term, keys_term), ("expert", "tensor"), "dp")
     columns = slot_rows
     grad_first = lax.psum_scatter(
         contract_rows(columns, grad_pre).astype(jnp.bfloat16), "dp", scatter_dimension=0, tiled=True

time: 504 us -> 718 us (1.42)
  waiting for transfers between devices: 232 us -> 444 us
    psum x1 -> x2, waiting for transfers between devices: 165 us -> 260 us  [_serve_records(): response = lax.psum(lax.psum(x_in, ax_name), mesh_ax)]
    reduce_scatter x1, waiting for transfers between devices: 0.01 us -> 78.9 us  [local(): lax.psum_scatter(contract_rows(columns, hidden).astype(jnp.bfloat16), 'dp...]
    reduce_scatter x1, waiting for transfers between devices: 0.01 us -> 37.7 us  [local(): lax.psum_scatter(contract_rows(columns, grad_pre).astype(jnp.bfloat16), '...]
    psum x1 -> x2, blocking collectives: 79.7 us -> 83.5 us  [_serve_records(): response = lax.psum(lax.psum(x_in, ax_name), mesh_ax)]
  transfers between devices with their start and end apart: 9 -> 10, of which waited for: 7 -> 9; matrix products, arithmetic and copies ran while one was open for 13% -> 9% of each run, Pallas kernels for 0% -> 0%
where the time goes in v1:
time: 718 us; the launch traced here: 716 us
  waiting for transfers between devices  444 us (62%)
  blocking collectives  122 us (17%)
  matrix products  62.7 us (9%)
  starting transfers between devices  32.3 us (4%)
  local copies, waits for them, and re-layouts  24.8 us (3%)
  other arithmetic  16.1 us (2%)
  between operations  14 us (2%)
    psum x2, waiting for transfers between devices, _serve_records(): response = lax.psum(lax.psum(x_in, ax_name), mesh_ax)  260 us
    psum x2, blocking collectives, _serve_records(): response = lax.psum(lax.psum(x_in, ax_name), mesh_ax)  83.5 us
    reduce_scatter x1, waiting for transfers between devices, local(): lax.psum_scatter(contract_rows(columns, hidden).astype(jnp.bfloat16), 'dp...  78.9 us
    reduce_scatter x1, waiting for transfers between devices, local(): lax.psum_scatter(contract_rows(columns, grad_pre).astype(jnp.bfloat16), '...  37.7 us
    all_to_all x1, waiting for transfers between devices, summed_on_arrival(): lax.all_to_all(tiles, axis, split_axis=0, concat_axis=0, tiled=True)  19.8 us
    all_to_all x1, blocking collectives, local(): lax.all_to_all(slot_inputs, 'expert', split_axis=1, concat_axis=0, tiled=...  19.4 us
    all_to_all x1, blocking collectives, from_everyone(): lax.all_to_all(jnp.broadcast_to(shard[None], (devices, *shard.shape)), ax...  18.9 us
    all_to_all x1, waiting for transfers between devices, local(): lax.all_to_all(grad_in_rows, 'expert', split_axis=0, concat_axis=1, tiled...  15.6 us
  transfers between devices with their start and end apart: 10, of which 9 were waited for; matrix products, arithmetic and copies ran while one was open for 9% of the time, Pallas kernels for 0%

profile of v1, /device:TPU:1, one launch (start us, length us, event | category | flops | bytes accessed | tf_op | source)
XLA Modules:
  0.0 716.1 jit_solution(10702119492185686737)
XLA Ops:
  22.6 10.0 %all-to-all-start = ((bf16[6,16,2,1280]{3,2,0,1:T(2,128)(2,1)}), bf16[6,16,2,1280]{3,2,0,1:T(2,128)(2,1)}, u32[]{:S(2)}, u32[]{:S(2)}) async-start(bf16[6,16,2,1280]{3,2,0,1:T(2,128)(2,1)} %copy.15), calls=%async_computation | async-start | bytes 983040 | tf_op jit(solution)/shard_map/all_to_all | solution.py:136
  34.4 4.6 convolution_convert_fusion.2
  43.2 6.1 all-to-all-done
  49.2 19.4 %all_to_all.80 = bf16[6,16,2,1280]{3,2,0,1:T(2,128)(2,1)S(1)} all-to-all(bf16[6,16,2,1280]{3,2,0,1:T(2,128)(2,1)} %copy.16), channel_id=1, replica_groups=mesh['dp'=8,'expert'=16,'tensor'=2] {'expert'}, dimensions={1} | all-to-all | bytes 983040 | tf_op jit(solution)/shard_map/all_to_all | solution.py:114
  69.2 18.9 %all_to_all.81 = bf16[2,96,1,2,1280]{4,3,2,1,0:T(2,128)(2,1)} all-to-all(bf16[2,96,1,2,1280]{4,3,2,1,0:T(2,128)(2,1)S(1)} %broadcast_in_dim.15), channel_id=1, replica_groups=mesh['dp'=8,'expert'=16,'tensor'=2] {'tensor'}, dimensions={0} | all-to-all | bytes 1966080 | tf_op jit(solution)/shard_map/all_to_all | solution.py:17
  90.6 4.6 all-to-all-start.1
  102.9 6.3 all-to-all-done.1
  112.5 4.9 fusion.33
  123.4 4.9 fusion.16
  128.3 8.3 %all-to-all-done.4 = bf16[2,192,1280]{2,1,0:T(8,128)(2,1)S(1)} async-done(((bf16[2,192,1280]{2,1,0:T(8,128)(2,1)}), bf16[2,192,1280]{2,1,0:T(8,128)(2,1)S(1)}, u32[]{:S(2)}, u32[]{:S(2)}) %all-to-all-start.4) | async-done | bytes 983072 | tf_op jit(solution)/shard_map/all_to_all | solution.py:46
  143.5 19.8 %all-to-all-done.6 = f32[2,192,1280]{2,1,0:T(8,128)S(1)} async-done(((f32[2,192,1280]{2,1,0:T(8,128)}), f32[2,192,1280]{2,1,0:T(8,128)S(1)}, u32[]{:S(2)}, u32[]{:S(2)}) %all-to-all-start.6) | async-done | bytes 1966112 | tf_op jit(solution)/shard_map/all_to_all | solution.py:40
  163.3 6.3 all-to-all-start.5
  170.7 15.6 %all-to-all-done.5 = bf16[96,1,2,1280]{3,2,1,0:T(2,128)(2,1)S(1)} async-done(((bf16[96,1,2,1280]{3,2,1,0:T(2,128)(2,1)}), bf16[96,1,2,1280]{3,2,1,0:T(2,128)(2,1)S(1)}, u32[]{:S(2)}, u32[]{:S(2)}) %all-to-all-start.5) | async-done | bytes 491552 | tf_op jit(solution)/shard_map/all_to_all | solution.py:145
  194.0 11.7 %all-to-all-done.7 = bf16[96,1,2,1280]{3,2,1,0:T(2,128)(2,1)S(1)} async-done(((bf16[96,1,2,1280]{3,2,1,0:T(2,128)(2,1)}), bf16[96,1,2,1280]{3,2,1,0:T(2,128)(2,1)S(1)}, u32[]{:S(2)}, u32[]{:S(2)}) %all-to-all-start.7) | async-done | bytes 491552 | tf_op jit(solution)/shard_map/all_to_all | solution.py:125
  212.9 260.0 %all-reduce.3.cloned.1.call-done = f32[1280,32]{0,1:T(8,128)} async-done(((f32[1280,32]{0,1:T(8,128)}), f32[1280,32]{0,1:T(8,128)}) %all-reduce.3.cloned.1.call-update) | async-done | bytes 163856 | tf_op jit(solution)/shard_map/psum | solution.py:11
  473.0 5.0 convolution_convert_fusion.1
  478.3 4.9 convolution_convert_fusion
  483.2 5.5 fusion.44
  488.7 10.6 %fusion.14 = (f32[1280]{0:T(1024)S(1)}, f32[6,256]{1,0:T(8,128)S(1)}, f32[6,256]{1,0:T(8,128)S(1)}, f32[6,256,1280]{2,1,0:T(8,128)}) fusion(bf16[6,256,1280]{2,1,0:T(8,128)(2,1)} %param.6, f32[6,256]{1,0:T(8,128)S(1)} %add_rsqrt_fusion, f32[6,256]{1,0:T(8,128)S(1)} %broadcast_multiply_fusion.2, f32[1280]{0:T(1024)S(1)} %copy-done.10, ...), kind=kOutput, calls=%fused_computation.16 | convolution fusion | flops 774631168 | bytes 19974144 | tf_op jit(solution)/shard_map/bmn,dn->bmd/dot_general | solution.py:82
  499.3 65.0 %psum.28 = f32[1280]{0:T(1024)S(1)} all-reduce(f32[1280]{0:T(1024)S(1)} %get-tuple-element.5), channel_id=1, replica_groups=mesh['dp'=8,'expert'=16,'tensor'=2] {'expert','tensor'}, use_global_device_ids=true, to_apply=%region_13.0 | all-reduce | flops 1280 | bytes 10240 | tf_op jit(solution)/shard_map/psum | solution.py:11
  564.3 18.5 %psum.29 = f32[1280]{0:T(1024)} all-reduce(f32[1280]{0:T(1024)S(1)} %psum.28), channel_id=1, replica_groups=mesh['dp'=8,'expert'=16,'tensor'=2] {'dp'}, use_global_device_ids=true, to_apply=%region_14.0 | all-reduce | flops 1280 | bytes 10240 | tf_op jit(solution)/shard_map/psum | solution.py:11
  582.8 8.6 %fusion.13 = bf16[6,256,1280]{2,1,0:T(8,128)(2,1)} fusion(bf16[6,256,1280]{2,1,0:T(8,128)(2,1)} %param.6, bf16[6,256,1280]{2,1,0:T(8,128)(2,1)} %param.7, f32[6,256,1280]{2,1,0:T(8,128)} %get-tuple-element.18, f32[6,256]{1,0:T(8,128)S(1)} %get-tuple-element.19, f32[6,256]{1,0:T(8,128)S(1)} %get-tuple-element.20, f32[1280]{0:T(1024)S(1)} %copy-done.10, ...), kind=kLoop, calls=%fused_computation.15 | loop fusion | flops 21626880 | bytes 19690496 | tf_op jit(solution)/shard_map/convert_element_type | solution.py:151
  591.4 37.7 %reduce-scatter.3.cloned.1.call-done = bf16[160,1280]{1,0:T(8,128)(2,1)} async-done(((bf16[1280,1280]{1,0:T(8,128)(2,1)}), bf16[160,1280]{1,0:T(8,128)(2,1)}) %reduce-scatter.3.cloned.1.call-update) | async-done | bytes 409616 | tf_op jit(solution)/shard_map/reduce_scatter | solution.py:154
  629.1 78.9 %reduce-scatter.5.cloned.1.call-done = bf16[160,1280]{1,0:T(8,128)(2,1)} async-done(((bf16[1280,1280]{1,0:T(8,128)(2,1)}), bf16[160,1280]{1,0:T(8,128)(2,1)}) %reduce-scatter.5.cloned.1.call-update) | async-done | bytes 409616 | tf_op jit(solution)/shard_map/reduce_scatter | solution.py:159
  (68 shorter events, 66.1 us)
Async XLA Ops:
  7.2 91.3 %copy-start = (bf16[1,1280,1280]{2,1,0:T(8,128)(2,1)S(1)}, bf16[1,1280,1280]{2,1,0:T(8,128)(2,1)}, u32[]{:S(2)}) copy-start(bf16[1,1280,1280]{2,1,0:T(8,128)(2,1)} %param.10) | copy-start | bytes 9830404
  7.2 3.4 copy-start.2
  7.2 4.6 copy-start.10
  7.2 4.6 copy-start.8
  13.6 0.7 copy-start.4
  22.6 26.6 %all-to-all-start = ((bf16[6,16,2,1280]{3,2,0,1:T(2,128)(2,1)}), bf16[6,16,2,1280]{3,2,0,1:T(2,128)(2,1)}, u32[]{:S(2)}, u32[]{:S(2)}) async-start(bf16[6,16,2,1280]{3,2,0,1:T(2,128)(2,1)} %copy.15), calls=%async_computation | async-start | bytes 983040 | tf_op jit(solution)/shard_map/all_to_all | solution.py:136
  90.6 18.6 %all-to-all-start.1 = ((bf16[2,96,1,2,1280]{4,3,2,1,0:T(2,128)(2,1)}), bf16[2,96,1,2,1280]{4,3,2,1,0:T(2,128)(2,1)}, u32[]{:S(2)}, u32[]{:S(2)}) async-start(bf16[2,96,1,2,1280]{4,3,2,1,0:T(2,128)(2,1)} %broadcast_in_dim.13), calls=%async_computation.1 | async-start | bytes 1966080 | tf_op jit(solution)/shard_map/all_to_all | solution.py:17
  117.4 2.4 copy-start.11
  119.8 16.8 %all-to-all-start.4 = ((bf16[2,192,1280]{2,1,0:T(8,128)(2,1)}), bf16[2,192,1280]{2,1,0:T(8,128)(2,1)S(1)}, u32[]{:S(2)}, u32[]{:S(2)}) async-start(bf16[2,192,1280]{2,1,0:T(8,128)(2,1)} %bitcast.77), calls=%async_computation.4 | async-start | bytes 1966080 | tf_op jit(solution)/shard_map/all_to_all | solution.py:46
  136.6 26.7 %all-to-all-start.6 = ((f32[2,192,1280]{2,1,0:T(8,128)}), f32[2,192,1280]{2,1,0:T(8,128)S(1)}, u32[]{:S(2)}, u32[]{:S(2)}) async-start(f32[2,192,1280]{2,1,0:T(8,128)} %fusion.16), calls=%async_computation.6 | async-start | bytes 3932160 | tf_op jit(solution)/shard_map/all_to_all | solution.py:40
  143.4 47.1 %copy-start.7 = (f32[6,256,32]{1,2,0:T(8,128)S(1)}, f32[6,256,32]{1,2,0:T(8,128)}, u32[]{:S(2)}) copy-start(f32[6,256,32]{1,2,0:T(8,128)} %get-tuple-element.9) | copy-start | bytes 589828
  163.3 22.9 %all-to-all-start.5 = ((bf16[96,1,2,1280]{3,2,1,0:T(2,128)(2,1)}), bf16[96,1,2,1280]{3,2,1,0:T(2,128)(2,1)S(1)}, u32[]{:S(2)}, u32[]{:S(2)}) async-start(bf16[96,1,2,1280]{3,2,1,0:T(2,128)(2,1)} %reshape.82), calls=%async_computation.5 | async-start | bytes 983040 | tf_op jit(solution)/shard_map/all_to_all | solution.py:145
  186.2 19.4 %all-to-all-start.7 = ((bf16[96,1,2,1280]{3,2,1,0:T(2,128)(2,1)}), bf16[96,1,2,1280]{3,2,1,0:T(2,128)(2,1)S(1)}, u32[]{:S(2)}, u32[]{:S(2)}) async-start(bf16[96,1,2,1280]{3,2,1,0:T(2,128)(2,1)} %convert_element_type.73), calls=%async_computation.7 | async-start | bytes 983040 | tf_op jit(solution)/shard_map/all_to_all | solution.py:125
  189.7 283.2 %all-reduce.3.cloned.1.call-start = ((), (), s32[]{:S(2)}) async-start(), calls=%async_computation.10 | async-start | bytes 327680 | tf_op jit(solution)/shard_map/psum | solution.py:11
  206.2 3.7 copy-start.3
  209.9 263.1 %copy-start.6 = (bf16[384,1280]{1,0:T(8,128)(2,1)S(1)}, bf16[384,1280]{1,0:T(8,128)(2,1)}, u32[]{:S(2)}) copy-start(bf16[384,1280]{1,0:T(8,128)(2,1)} %reshape_reshape.7) | copy-start | bytes 2949124
  212.8 378.6 %all-reduce.5.cloned.1.call-start = ((), (), s32[]{:S(2)}) async-start(), calls=%async_computation.11 | async-start | bytes 327680 | tf_op jit(solution)/shard_map/psum | solution.py:11
  472.9 5.4 copy-start.5
  472.9 156.2 %reduce-scatter.3.cloned.1.call-start = ((), (), s32[]{:S(2)}) async-start(), calls=%async_computation.12 | async-start | bytes 3686400 | tf_op jit(solution)/shard_map/reduce_scatter | solution.py:154
  478.0 230.0 %reduce-scatter.5.cloned.1.call-start = ((), (), s32[]{:S(2)}) async-start(), calls=%async_computation.13 | async-start | bytes 3686400 | tf_op jit(solution)/shard_map/reduce_scatter | solution.py:159
  483.2 5.5 copy-start.9
  582.8 126.8 %copy-start.1 = (bf16[1,1280,1280]{2,1,0:T(8,128)(2,1)S(1)}, bf16[1,1280,1280]{2,1,0:T(8,128)(2,1)}, u32[]{:S(2)}) copy-start(bf16[1,1280,1280]{2,1,0:T(8,128)(2,1)} %param.10) | copy-start | bytes 9830404
Sparse Core Ops, SparseCore 0:
  212.9 259.9 all-reduce.2
  475.5 69.3 all-reduce.4
  548.1 81.0 reduce-scatter.2
  632.1 75.8 reduce-scatter.4
